TPU v7x, 32 devices: a whole 2x2x4 slice. The times are simulated.
32 devices in a mesh: seq: 8 (over z, x), head: 4 (over y, core).
Axes of the slice: x: 2, y: 2, z: 4, core: 2. Of those that a mesh axis runs over, the one named last changes fastest.
Arguments:
- video_q: bfloat16 [1024, 4096], P(('seq', 'head')), may hold values from -200 to 200
- video_k: bfloat16 [1024, 4096], P(('seq', 'head')), may hold values from -6 to 6
- video_v: bfloat16 [1024, 4096], P(('seq', 'head')), may hold values from -6 to 6
- text_k: bfloat16 [512, 4096], P(None, 'head'), may hold values from -6 to 6
- text_v: bfloat16 [512, 4096], P(None, 'head'), may hold values from -6 to 6
- out_weight: bfloat16 [4096, 5120], P('head'), may hold values from -0.09375 to 0.09375
Outputs:
- video_out: bfloat16 [1024, 5120], P(('seq', 'head'))
All inputs are finite; a program needn't handle non-finite values.
Results may differ from a plain program's by a relative error of at most 0.018.
Values may be sent and summed in bfloat16 or wider, within the bound.
A program may use at most 128 MiB of HBM per device.

v0:
```python
import jax
import jax.numpy as jnp
from jax import lax
from jax.sharding import PartitionSpec as P

HD = 128


def as_heads(array):
    return array.reshape(array.shape[0], array.shape[1] // HD, HD)


def scores_of(query_heads, key_heads):
    return jnp.einsum(
        "qhd,khd->hqk", query_heads, key_heads, preferred_element_type=jnp.float32
    ) * HD ** (-0.5)


def weigh_values(scores, row_max, value_heads):
    weights = jnp.exp(scores - row_max[..., None]).astype(jnp.bfloat16)
    totals = jnp.sum(weights.astype(jnp.float32), axis=2)
    summed = jnp.einsum("hqk,khd->hqd", weights, value_heads, preferred_element_type=jnp.float32)
    return (totals, summed)


def local_partial(query_heads, key_heads, value_heads):
    scores = scores_of(query_heads, key_heads)
    row_max = jnp.max(scores, axis=2)
    totals, summed = weigh_values(scores, row_max, value_heads)
    return (row_max, totals, summed)


def combine_partial(first, second):
    joint = jnp.maximum(first[0], second[0])
    first_factor = jnp.exp(first[0] - joint)
    second_factor = jnp.exp(second[0] - joint)
    totals = first[1] * first_factor + second[1] * second_factor
    summed = first[2] * first_factor[..., None] + second[2] * second_factor[..., None]
    return (joint, totals, summed)


def body(video_q, video_k, video_v, text_k, text_v, out_weight):
    queries, key_rows, value_rows = (
        lax.all_to_all(video_q, "head", split_axis=1, concat_axis=0, tiled=True),
        lax.all_to_all(video_k, "head", split_axis=1, concat_axis=0, tiled=True),
        lax.all_to_all(video_v, "head", split_axis=1, concat_axis=0, tiled=True),
    )
    rows_here = queries.shape[0]
    query_heads = as_heads(queries)
    text_part = local_partial(query_heads, as_heads(text_k), as_heads(text_v))
    merged = combine_partial(
        text_part,
        local_partial(
            query_heads,
            as_heads(lax.all_gather(key_rows, "seq", axis=0, tiled=True)),
            as_heads(lax.all_gather(value_rows, "seq", axis=0, tiled=True)),
        ),
    )
    normalized = merged[2] / merged[1][..., None]
    attended = normalized.transpose(1, 0, 2).reshape(rows_here, -1).astype(jnp.bfloat16)
    return lax.psum_scatter(
        jnp.dot(attended, out_weight, preferred_element_type=jnp.float32).astype(jnp.bfloat16),
        "head",
        scatter_dimension=0,
        tiled=True,
    )


def solution(mesh):
    in_specs = (
        P(("seq", "head"), None),
        P(("seq", "head"), None),
        P(("seq", "head"), None),
        P(None, "head"),
        P(None, "head"),
        P("head", None),
    )
    out_specs = P(("seq", "head"), None)
    return jax.shard_map(body, mesh=mesh, in_specs=in_specs, out_specs=out_specs, check_vma=False)
```

profile of v0, /device:TPU:0, one launch (start us, length us, event | category | flops | bytes accessed | tf_op | source)
XLA Modules:
  0.0 162.2 jit_solution(479309963512354271)
XLA Ops:
  6.5 0.0 copy-start
  6.5 0.0 copy-start.4
  6.5 0.0 copy-start.3
  6.5 0.0 all-gather.3.cloned.1.call-start
  6.5 1.1 copy.63
  7.7 10.2 %all_to_all.54 = bf16[32,4,1024]{2,0,1:T(8,128)(2,1)} all-to-all(bf16[32,4,1024]{2,0,1:T(8,128)(2,1)S(1)} %bitcast.80), channel_id=1, replica_groups=mesh['seq'=8,'head'=4] {'head'}, dimensions={1} | all-to-all | bytes 524288 | tf_op jit(solution)/shard_map/all_to_all | solution.py:45
  17.8 0.0 all-gather.3.cloned.1.call-update
  17.9 0.0 all-gather.5.cloned.1.call-start
  17.9 1.0 copy.62
  18.9 9.1 %all_to_all.55 = bf16[32,4,1024]{2,0,1:T(8,128)(2,1)} all-to-all(bf16[32,4,1024]{2,0,1:T(8,128)(2,1)S(1)} %bitcast.81), channel_id=1, replica_groups=mesh['seq'=8,'head'=4] {'head'}, dimensions={1} | all-to-all | bytes 524288 | tf_op jit(solution)/shard_map/all_to_all | solution.py:46
  28.0 0.0 all-gather.5.cloned.1.call-update
  28.0 0.0 copy-done.4
  28.0 0.7 copy.64
  28.7 3.4 %all-to-all-start = ((bf16[32,4,1024]{2,0,1:T(8,128)(2,1)}), bf16[32,4,1024]{2,0,1:T(8,128)(2,1)S(1)}, u32[]{:S(2)}, u32[]{:S(2)}) async-start(bf16[32,4,1024]{2,0,1:T(8,128)(2,1)} %bitcast.71), calls=%async_computation | async-start | bytes 524288 | tf_op jit(solution)/shard_map/all_to_all | solution.py:44
  32.1 0.0 reduce-scatter.2.cloned.1.call-start
  32.2 0.0 copy-done.3
  32.2 1.3 copy.39
  33.5 4.6 %all-to-all-done = bf16[32,4,1024]{2,0,1:T(8,128)(2,1)S(1)} async-done(((bf16[32,4,1024]{2,0,1:T(8,128)(2,1)}), bf16[32,4,1024]{2,0,1:T(8,128)(2,1)S(1)}, u32[]{:S(2)}, u32[]{:S(2)}) %all-to-all-start) | async-done | bytes 262176 | tf_op jit(solution)/shard_map/all_to_all | solution.py:44
  38.2 0.0 copy-done
  38.2 0.5 multiply_reduce_fusion.1
  38.7 0.6 convert_reduce_fusion.1
  39.3 28.5 %all-gather.3.cloned.1.call-done = bf16[1024,1024]{1,0:T(8,128)(2,1)} async-done(((bf16[128,1024]{1,0:T(8,128)(2,1)}), bf16[1024,1024]{1,0:T(8,128)(2,1)}) %all-gather.3.cloned.1.call-update) | async-done | bytes 2097168 | tf_op jit(solution)/shard_map/all_gather | solution.py:55
  67.8 3.9 %copy.33 = bf16[1024,1024]{0,1:T(8,128)(2,1)} copy(bf16[1024,1024]{1,0:T(8,128)(2,1)} %all-gather.3.cloned.1.call-done) | data formatting | bytes 4194304 | tf_op jit(solution)/shard_map/all_gather | solution.py:55
  71.7 2.4 %multiply_reduce_fusion = (f32[8,128]{1,0:T(8,128)S(1)}, f32[8,128,1024]{2,1,0:T(8,128)S(1)}) fusion(bf16[1024,8,128]{0,2,1:T(8,128)(2,1)} %bitcast.72, bf16[128,8,128]{2,1,0:T(8,128)(2,1)S(1)} %bitcast.75), kind=kOutput, calls=%fused_computation.3 | convolution fusion | flops 270531584 | bytes 6557696 | tf_op jit(solution)/shard_map/qhd,khd->hqk/dot_general | solution.py:14
  74.1 0.0 copy-start.1
  74.1 0.0 copy-start.2
  74.1 0.9 convert_reduce_fusion
  75.0 1.0 copy-done.1
  76.0 0.1 copy-done.2
  76.1 1.4 fusion
  77.5 40.0 %all-gather.5.cloned.1.call-done = bf16[1024,1024]{1,0:T(8,128)(2,1)} async-done(((bf16[128,1024]{1,0:T(8,128)(2,1)}), bf16[1024,1024]{1,0:T(8,128)(2,1)}) %all-gather.5.cloned.1.call-update) | async-done | bytes 2097168 | tf_op jit(solution)/shard_map/all_gather | solution.py:56
  117.6 2.9 %copy.37 = bf16[1024,1024]{0,1:T(8,128)(2,1)S(1)} copy(bf16[1024,1024]{1,0:T(8,128)(2,1)} %all-gather.5.cloned.1.call-done) | data formatting | bytes 4194304 | tf_op jit(solution)/shard_map/all_gather | solution.py:56
  120.4 3.4 %fusion.4 = bf16[128,8,128]{0,2,1:T(8,128)(2,1)S(1)} fusion(f32[128,8,128]{0,2,1:T(8,128)} %fusion, bf16[1024,8,128]{0,2,1:T(8,128)(2,1)S(1)} %bitcast.76, f32[8,128,1024]{2,1,0:T(8,128)} %copy-done.1, f32[8,128]{1,0:T(8,128)S(1)} %get-tuple-element.8, f32[128,8]{0,1:T(8,128)S(1)} %get-tuple-element.5, f32[128,8]{0,1:T(8,128)S(1)} %get-tuple-element.6), kind=kOutput, calls=%fused_computation.13 | convolution fusion | flops 272105472 | bytes 7090176 | tf_op jit(solution)/shard_map/hqk,khd->hqd/dot_general | solution.py:22
  123.8 6.6 %convolution_convert_fusion = bf16[128,5120]{1,0:T(8,128)(2,1)} fusion(bf16[128,1024]{0,1:T(8,128)(2,1)S(1)} %bitcast.82, bf16[1024,5120]{1,0:T(8,128)(2,1)} %param.11), kind=kOutput, calls=%fused_computation | convolution fusion | flops 1342832640 | bytes 12058624 | tf_op jit(solution)/shard_map/dot_general | solution.py:62
  130.5 0.0 reduce-scatter.2.cloned.1.call-update
  130.5 25.1 %reduce-scatter.2.cloned.1.call-done = bf16[32,5120]{1,0:T(8,128)(2,1)} async-done(((bf16[128,5120]{1,0:T(8,128)(2,1)}), bf16[32,5120]{1,0:T(8,128)(2,1)}) %reduce-scatter.2.cloned.1.call-update) | async-done | bytes 327696 | tf_op jit(solution)/shard_map/reduce_scatter | solution.py:61
  (2 shorter events, 0.1 us)
Async XLA Ops:
  6.5 31.6 %copy-start = (bf16[512,1024]{1,0:T(8,128)(2,1)S(1)}, bf16[512,1024]{1,0:T(8,128)(2,1)}, u32[]{:S(2)}) copy-start(bf16[512,1024]{1,0:T(8,128)(2,1)} %param.9) | copy-start | bytes 3145732
  6.5 21.5 %copy-start.4 = (bf16[32,4096]{1,0:T(8,128)(2,1)S(1)}, bf16[32,4096]{1,0:T(8,128)(2,1)}, u32[]{:S(2)}) copy-start(bf16[32,4096]{1,0:T(8,128)(2,1)} %param.6) | copy-start | bytes 786436
  6.5 25.7 %copy-start.3 = (bf16[512,1024]{1,0:T(8,128)(2,1)S(1)}, bf16[512,1024]{1,0:T(8,128)(2,1)}, u32[]{:S(2)}) copy-start(bf16[512,1024]{1,0:T(8,128)(2,1)} %param.10) | copy-start | bytes 3145732
  6.5 61.2 %all-gather.3.cloned.1.call-start = ((), (), s32[]{:S(2)}) async-start(), calls=%async_computation.4 | async-start | bytes 2359296 | tf_op jit(solution)/shard_map/all_gather | solution.py:55
  17.9 99.7 %all-gather.5.cloned.1.call-start = ((), (), s32[]{:S(2)}) async-start(), calls=%async_computation.5 | async-start | bytes 2359296 | tf_op jit(solution)/shard_map/all_gather | solution.py:56
  28.7 9.4 %all-to-all-start = ((bf16[32,4,1024]{2,0,1:T(8,128)(2,1)}), bf16[32,4,1024]{2,0,1:T(8,128)(2,1)S(1)}, u32[]{:S(2)}, u32[]{:S(2)}) async-start(bf16[32,4,1024]{2,0,1:T(8,128)(2,1)} %bitcast.71), calls=%async_computation | async-start | bytes 524288 | tf_op jit(solution)/shard_map/all_to_all | solution.py:44
  32.1 123.5 %reduce-scatter.2.cloned.1.call-start = ((), (), s32[]{:S(2)}) async-start(), calls=%async_computation.6 | async-start | bytes 1638400 | tf_op jit(solution)/shard_map/reduce_scatter | solution.py:61
  74.1 1.9 %copy-start.1 = (f32[8,128,1024]{2,1,0:T(8,128)}, f32[8,128,1024]{2,1,0:T(8,128)S(1)}, u32[]{:S(2)}) copy-start(f32[8,128,1024]{2,1,0:T(8,128)S(1)} %get-tuple-element.9) | copy-start | bytes 12582916
  74.1 2.0 %copy-start.2 = (bf16[512,1024]{0,1:T(8,128)(2,1)S(1)}, bf16[512,1024]{0,1:T(8,128)(2,1)}, u32[]{:S(2)}) copy-start(bf16[512,1024]{0,1:T(8,128)(2,1)} %copy.39) | copy-start | bytes 3145732
Sparse Core Ops, SparseCore 0:
  18.0 49.7 all-gather.2
  69.9 47.6 all-gather.4
  130.6 24.9 reduce-scatter.1
where the time goes:
time: 163 us; the launch traced here: 162 us
  waiting for transfers between devices  98.2 us (60%)
  blocking collectives  19.3 us (12%)
  matrix products  14.4 us (9%)
  between operations  13.2 us (8%)
  local copies, waits for them, and re-layouts  12 us (7%)
  starting transfers between devices  3.49 us (2%)
    all_gather x1, waiting for transfers between devices, body(): lax.all_gather(value_rows, 'seq', axis=0, tiled=True)  40 us
    all_gather x1, waiting for transfers between devices, body(): lax.all_gather(key_rows, 'seq', axis=0, tiled=True)  28.5 us
    reduce_scatter x1, waiting for transfers between devices, body(): lax.psum_scatter(jnp.dot(attended, out_weight, preferred_element_type=jnp...  25.1 us
    all_to_all x1, blocking collectives, body(): lax.all_to_all(video_k, 'head', split_axis=1, concat_axis=0, tiled=True)  10.2 us
    all_to_all x1, blocking collectives, body(): lax.all_to_all(video_v, 'head', split_axis=1, concat_axis=0, tiled=True)  9.08 us
    dot_general x1, matrix products, body(): jnp.dot(attended, out_weight, preferred_element_type=jnp.float32)  6.62 us
    dot_general x2, matrix products, weigh_values(): jnp.einsum('hqk,khd->hqd', weights, value_heads, preferred_element_type=j...  4.87 us
    all_to_all x1, waiting for transfers between devices, body(): lax.all_to_all(video_q, 'head', split_axis=1, concat_axis=0, tiled=True)  4.57 us
  transfers between devices with their start and end apart: 4, of which 4 were waited for; matrix products, arithmetic and copies ran while one was open for 8% of the time, Pallas kernels for 0%

commit v1 on v0

--- a/solution.py
+++ b/solution.py
@@ -43,7 +43,12 @@
     queries, key_rows, value_rows = (
         lax.all_to_all(video_q, "head", split_axis=1, concat_axis=0, tiled=True),
         lax.all_to_all(video_k, "head", split_axis=1, concat_axis=0, tiled=True),
-        lax.all_to_all(video_v, "head", split_axis=1, concat_axis=0, tiled=True),
+        jnp.concatenate(
+            lax.all_to_all(
+                jnp.stack(jnp.split(video_v, lax.axis_size("head"), axis=1)), "head", 0, 0
+            ),
+            axis=0,
+        ),
     )
     rows_here = queries.shape[0]
     query_heads = as_heads(queries)

time: 163 us -> 161 us (0.988)
  local copies, waits for them, and re-layouts: 12 us -> 10 us
    all_gather x1 -> x0, local copies, waits for them, and re-layouts: 2.85 us -> none  [body(): lax.all_gather(value_rows, 'seq', axis=0, tiled=True)]
  transfers between devices with their start and end apart: 4 -> 4, of which waited for: 4 -> 4; matrix products, arithmetic and copies ran while one was open for 8% -> 9% of each run, Pallas kernels for 0% -> 0%
where the time goes in v1:
time: 161 us
  waiting for transfers between devices  98.8 us (61%)
  blocking collectives  18.7 us (12%)
  matrix products  15 us (9%)
  between operations  13.2 us (8%)
  local copies, waits for them, and re-layouts  10 us (6%)
  starting transfers between devices  3.49 us (2%)
    all_gather x1, waiting for transfers between devices, body(): lax.all_gather(value_rows, 'seq', axis=0, tiled=True)  41.2 us
    all_gather x1, waiting for transfers between devices, body(): lax.all_gather(key_rows, 'seq', axis=0, tiled=True)  28.3 us
    reduce_scatter x1, waiting for transfers between devices, body(): lax.psum_scatter(jnp.dot(attended, out_weight, preferred_element_type=jnp...  24.8 us
    all_to_all x1, blocking collectives, body(): lax.all_to_all(video_k, 'head', split_axis=1, concat_axis=0, tiled=True)  10.3 us
    all_to_all x1, blocking collectives, body(): lax.all_to_all(jnp.stack(jnp.split(video_v, lax.axis_size('head'), axis=1...  8.39 us
    dot_general x1, matrix products, body(): jnp.dot(attended, out_weight, preferred_element_type=jnp.float32)  6.62 us
    dot_general x2, matrix products, weigh_values(): jnp.einsum('hqk,khd->hqd', weights, value_heads, preferred_element_type=j...  5.45 us
    all_to_all x1, waiting for transfers between devices, body(): lax.all_to_all(video_q, 'head', split_axis=1, concat_axis=0, tiled=True)  4.58 us
  transfers between devices with their start and end apart: 4, of which 4 were waited for; matrix products, arithmetic and copies ran while one was open for 9% of the time, Pallas kernels for 0%

profile of v1, /device:TPU:0, one launch (start us, length us, event | category | flops | bytes accessed | tf_op | source)
XLA Modules:
  0.0 160.8 jit_solution(2538283910031757952)
XLA Ops:
  6.5 0.0 copy-start
  6.5 0.0 copy-start.4
  6.5 0.0 all-gather.3.cloned.1.call-start
  6.5 1.1 copy.58
  7.6 0.0 copy-start.3
  7.6 10.3 %all_to_all.40 = bf16[32,4,1024]{2,0,1:T(8,128)(2,1)} all-to-all(bf16[32,4,1024]{2,0,1:T(8,128)(2,1)S(1)} %bitcast.81), channel_id=1, replica_groups=mesh['seq'=8,'head'=4] {'head'}, dimensions={1} | all-to-all | bytes 524288 | tf_op jit(solution)/shard_map/all_to_all | solution.py:45
  17.9 0.0 all-gather.3.cloned.1.call-update
  18.0 0.0 all-gather.5.cloned.1.call-start
  18.0 1.0 slice_bitcast_fusion.3
  19.0 8.4 %all_to_all.41 = bf16[4,32,1024]{2,1,0:T(8,128)(2,1)S(1)} all-to-all(bf16[4,32,1024]{2,1,0:T(8,128)(2,1)S(1)} %pad_maximum_fusion), channel_id=1, replica_groups=mesh['seq'=8,'head'=4] {'head'}, dimensions={0} | all-to-all | bytes 524288 | tf_op jit(solution)/shard_map/all_to_all | solution.py:47
  27.4 0.8 copy.35
  28.2 0.0 all-gather.5.cloned.1.call-update
  28.3 0.0 copy-done.4
  28.3 0.7 copy.59
  29.0 3.4 %all-to-all-start = ((bf16[32,4,1024]{2,0,1:T(8,128)(2,1)}), bf16[32,4,1024]{2,0,1:T(8,128)(2,1)S(1)}, u32[]{:S(2)}, u32[]{:S(2)}) async-start(bf16[32,4,1024]{2,0,1:T(8,128)(2,1)} %bitcast.73), calls=%async_computation | async-start | bytes 524288 | tf_op jit(solution)/shard_map/all_to_all | solution.py:44
  32.4 0.0 reduce-scatter.2.cloned.1.call-start
  32.5 0.0 copy-done.3
  32.5 1.3 copy.37
  33.8 4.6 %all-to-all-done = bf16[32,4,1024]{2,0,1:T(8,128)(2,1)S(1)} async-done(((bf16[32,4,1024]{2,0,1:T(8,128)(2,1)}), bf16[32,4,1024]{2,0,1:T(8,128)(2,1)S(1)}, u32[]{:S(2)}, u32[]{:S(2)}) %all-to-all-start) | async-done | bytes 262176 | tf_op jit(solution)/shard_map/all_to_all | solution.py:44
  38.4 0.0 copy-done
  38.5 0.5 multiply_reduce_fusion.1
  39.0 0.6 convert_reduce_fusion.1
  39.6 28.3 %all-gather.3.cloned.1.call-done = bf16[1024,1024]{1,0:T(8,128)(2,1)} async-done(((bf16[128,1024]{1,0:T(8,128)(2,1)}), bf16[1024,1024]{1,0:T(8,128)(2,1)}) %all-gather.3.cloned.1.call-update) | async-done | bytes 2097168 | tf_op jit(solution)/shard_map/all_gather | solution.py:60
  67.9 3.9 %copy.32 = bf16[1024,1024]{0,1:T(8,128)(2,1)} copy(bf16[1024,1024]{1,0:T(8,128)(2,1)} %all-gather.3.cloned.1.call-done) | data formatting | bytes 4194304 | tf_op jit(solution)/shard_map/all_gather | solution.py:60
  71.8 2.4 %multiply_reduce_fusion = (f32[8,128]{1,0:T(8,128)S(1)}, f32[8,128,1024]{2,1,0:T(8,128)S(1)}) fusion(bf16[1024,8,128]{0,2,1:T(8,128)(2,1)} %bitcast.74, bf16[128,8,128]{2,1,0:T(8,128)(2,1)S(1)} %bitcast.77), kind=kOutput, calls=%fused_computation.3 | convolution fusion | flops 270531584 | bytes 6557696 | tf_op jit(solution)/shard_map/qhd,khd->hqk/dot_general | solution.py:14
  74.2 0.0 copy-start.1
  74.2 0.0 copy-start.2
  74.2 0.9 convert_reduce_fusion
  75.1 1.0 copy-done.1
  76.1 0.1 copy-done.2
  76.2 1.4 fusion
  77.6 41.2 %all-gather.5.cloned.1.call-done = bf16[1024,1024]{0,1:T(8,128)(2,1)} async-done(((bf16[128,1024]{0,1:T(8,128)(2,1)}), bf16[1024,1024]{0,1:T(8,128)(2,1)}) %all-gather.5.cloned.1.call-update) | async-done | bytes 2097168 | tf_op jit(solution)/shard_map/all_gather | solution.py:61
  118.8 4.0 %fusion.4 = bf16[128,8,128]{0,2,1:T(8,128)(2,1)S(1)} fusion(f32[128,8,128]{0,2,1:T(8,128)} %fusion, bf16[1024,8,128]{0,2,1:T(8,128)(2,1)} %bitcast.85, f32[8,128,1024]{2,1,0:T(8,128)} %copy-done.1, f32[8,128]{1,0:T(8,128)S(1)} %get-tuple-element.12, f32[128,8]{0,1:T(8,128)S(1)} %get-tuple-element.5, f32[128,8]{0,1:T(8,128)S(1)} %get-tuple-element.6), kind=kOutput, calls=%fused_computation.13 | convolution fusion | flops 272105472 | bytes 7090176 | tf_op jit(solution)/shard_map/hqk,khd->hqd/dot_general | solution.py:22
  122.8 6.6 %convolution_convert_fusion = bf16[128,5120]{1,0:T(8,128)(2,1)} fusion(bf16[128,1024]{0,1:T(8,128)(2,1)S(1)} %bitcast.82, bf16[1024,5120]{1,0:T(8,128)(2,1)} %param.11), kind=kOutput, calls=%fused_computation | convolution fusion | flops 1342832640 | bytes 12058624 | tf_op jit(solution)/shard_map/dot_general | solution.py:67
  129.4 0.0 reduce-scatter.2.cloned.1.call-update
  129.5 24.8 %reduce-scatter.2.cloned.1.call-done = bf16[32,5120]{1,0:T(8,128)(2,1)} async-done(((bf16[128,5120]{1,0:T(8,128)(2,1)}), bf16[32,5120]{1,0:T(8,128)(2,1)}) %reduce-scatter.2.cloned.1.call-update) | async-done | bytes 327696 | tf_op jit(solution)/shard_map/reduce_scatter | solution.py:66
  (3 shorter events, 0.1 us)
Async XLA Ops:
  6.5 31.9 %copy-start = (bf16[512,1024]{1,0:T(8,128)(2,1)S(1)}, bf16[512,1024]{1,0:T(8,128)(2,1)}, u32[]{:S(2)}) copy-start(bf16[512,1024]{1,0:T(8,128)(2,1)} %param.9) | copy-start | bytes 3145732
  6.5 21.7 %copy-start.4 = (bf16[32,4096]{1,0:T(8,128)(2,1)S(1)}, bf16[32,4096]{1,0:T(8,128)(2,1)}, u32[]{:S(2)}) copy-start(bf16[32,4096]{1,0:T(8,128)(2,1)} %param.6) | copy-start | bytes 786436
  6.5 61.3 %all-gather.3.cloned.1.call-start = ((), (), s32[]{:S(2)}) async-start(), calls=%async_computation.4 | async-start | bytes 2359296 | tf_op jit(solution)/shard_map/all_gather | solution.py:60
  7.6 24.9 %copy-start.3 = (bf16[512,1024]{1,0:T(8,128)(2,1)S(1)}, bf16[512,1024]{1,0:T(8,128)(2,1)}, u32[]{:S(2)}) copy-start(bf16[512,1024]{1,0:T(8,128)(2,1)} %param.10) | copy-start | bytes 3145732
  18.0 100.8 %all-gather.5.cloned.1.call-start = ((), (), s32[]{:S(2)}) async-start(), calls=%async_computation.5 | async-start | bytes 2359296 | tf_op jit(solution)/shard_map/all_gather | solution.py:61
  29.0 9.4 %all-to-all-start = ((bf16[32,4,1024]{2,0,1:T(8,128)(2,1)}), bf16[32,4,1024]{2,0,1:T(8,128)(2,1)S(1)}, u32[]{:S(2)}, u32[]{:S(2)}) async-start(bf16[32,4,1024]{2,0,1:T(8,128)(2,1)} %bitcast.73), calls=%async_computation | async-start | bytes 524288 | tf_op jit(solution)/shard_map/all_to_all | solution.py:44
  32.4 121.8 %reduce-scatter.2.cloned.1.call-start = ((), (), s32[]{:S(2)}) async-start(), calls=%async_computation.6 | async-start | bytes 1638400 | tf_op jit(solution)/shard_map/reduce_scatter | solution.py:66
  74.2 1.9 %copy-start.1 = (f32[8,128,1024]{2,1,0:T(8,128)}, f32[8,128,1024]{2,1,0:T(8,128)S(1)}, u32[]{:S(2)}) copy-start(f32[8,128,1024]{2,1,0:T(8,128)S(1)} %get-tuple-element.13) | copy-start | bytes 12582916
  74.2 2.0 %copy-start.2 = (bf16[512,1024]{0,1:T(8,128)(2,1)S(1)}, bf16[512,1024]{0,1:T(8,128)(2,1)}, u32[]{:S(2)}) copy-start(bf16[512,1024]{0,1:T(8,128)(2,1)} %copy.37) | copy-start | bytes 3145732
Sparse Core Ops, SparseCore 0:
  18.1 49.7 all-gather.2
  69.9 48.8 all-gather.4
  129.6 24.5 reduce-scatter.1
